TPU v7x, 32 devices: a whole 2x2x4 slice. The times are simulated.
32 devices in a mesh: pair: 4 (over y, x), side: 2 (over core), blk: 4 (over z).
Axes of the slice: x: 2, y: 2, z: 4, core: 2. Of those that a mesh axis runs over, the one named last changes fastest.
Arguments:
- intersect: float32 [4096, 768], P(('pair', 'side', 'blk')), parts along dimension 0, may hold values from -0.1 to 1.7, as said below
- half_factors: float32 [4096, 384], P(('pair', 'side', 'blk')), parts along dimension 0, may hold values from -0.03 to 1.35, as said below
- z_pattern: int32 [32, 6], P(('pair', 'side', 'blk')), parts along dimension 0, may hold values 0 or 1
Outputs:
- refined_factor: float32 [4096, 768], P(('pair', 'side', 'blk')), parts along dimension 0
There are 4 independent parts, one for each index of `pair`. A program takes and returns all parts, laid end to end along the dimension named above; each array names one. Nothing has to cross between parts.
Inputs may be any that keep to these rules, and one draw needn't show every extreme that they name: As a whole windowed matrix, intersect is symmetric: S[a, b] = S[b, a]. `half_factors`: entries of the other half and outside the grid of blocks are absent or zero. `z_pattern`: 1 keeps a tile of the factor, 0 drops it; diagonal tiles are kept whatever it says.
All inputs are finite; a program needn't handle non-finite values. No bound on the sum of `z_pattern` on one device may be relied on, other than what follows from the above.
Results may differ from a plain program's by a relative error of at most 0.0001.
Values sent between devices are 32-bit elements; how exact they have to be, the bound alone decides.
A program may use at most 64 MiB of HBM per device.

v0:
```python
import jax
import jax.numpy as jnp
from jax import lax
from jax.sharding import PartitionSpec as P

ITERS = 2


def padded(cells, sides, width):
    for axis, dim in sides:
        count = lax.axis_size(axis)
        ends = count - 1
        head = lax.slice_in_dim(cells, 0, width, axis=dim)
        tail = lax.slice_in_dim(cells, cells.shape[dim] - width, cells.shape[dim], axis=dim)
        cells = jnp.concatenate(
            [
                lax.ppermute(tail, axis, [(i, (i + 1) % count) for i in range(ends)]),
                cells,
                lax.ppermute(head, axis, [((i + 1) % count, i) for i in range(ends)]),
            ],
            axis=dim,
        )
    return cells


def swapped(block, axis, stride):
    count = lax.axis_size(axis)
    route = []
    for low in range(count):
        high = low | 1 << stride
        if high != low and high < count:
            route += [(low, high), (high, low)]
    return lax.ppermute(block, axis, route)


def near_blocks(panel):
    return padded(panel[None], (("blk", 0),), 1)


def neighbours(panel):
    side = lax.axis_index("side")
    local = near_blocks(panel)
    other = swapped(local, "side", 0)
    return jnp.stack((jnp.where(side == 0, local, other), jnp.where(side == 0, other, local)))


def window_product(left, nearby):
    outputs = []
    for target in range(3):
        total = None
        for slot in range(3):
            source = target + 1 - slot
            if 0 <= source <= 2:
                term = lax.dot_general(
                    left[:, slot],
                    nearby[:, slot, :, source],
                    (((1, 2), (0, 1)), ((), ())),
                    precision=lax.Precision.HIGHEST,
                    preferred_element_type=jnp.float32,
                )
                total = term if total is None else total + term
        outputs.append(total)
    return jnp.stack(outputs, axis=1)


def window_cross(near_factor, near_image, side):
    mines = []
    for slot in range(3):
        column = near_factor[:, slot, :, 2 - slot]
        mines.append(lax.dynamic_index_in_dim(column, side, axis=2, keepdims=False))
    outputs = []
    for target in range(3):
        total = None
        for slot in range(3):
            source = target + 1 - slot
            if 0 <= source <= 2:
                term = lax.dot_general(
                    mines[slot],
                    near_image[:, slot, :, source],
                    (((0, 1), (0, 1)), ((), ())),
                    precision=lax.Precision.HIGHEST,
                    preferred_element_type=jnp.float32,
                )
                total = term if total is None else total + term
        outputs.append(total)
    return jnp.stack(outputs, axis=1)


def window_keep(pattern, tile, side):
    count = pattern.shape[0]
    grid = pattern.reshape(count, 3, 2, count)
    slots = jnp.arange(3)[None, :, None, None]
    halves = jnp.arange(2)[None, None, :, None]
    row_tiles = jnp.arange(count)[:, None, None, None]
    col_tiles = jnp.arange(count)[None, None, None, :]
    diagonal = ((slots == 1) & (halves == side) & (row_tiles == col_tiles)).astype(jnp.int32)
    kept = jnp.maximum(grid, diagonal).astype(jnp.float32)
    wide = jnp.broadcast_to(kept[:, None, :, :, :, None], (count, tile, 3, 2, count, tile))
    return wide.reshape(count * tile, 3, 2, count * tile)


def per_device(intersect, half_factors, z_pattern):
    rows = intersect.shape[0]
    tile = rows // z_pattern.shape[0]
    side = lax.axis_index("side")
    eye_side = jnp.eye(2, dtype=jnp.float32)
    own_side = (jnp.arange(2) == side).astype(jnp.float32)
    intersect_win = intersect.reshape(rows, 3, 2, rows)
    keep = window_keep(z_pattern, tile, side)
    slots = jnp.arange(3)[None, :, None, None]
    halves = jnp.arange(2)[None, None, :, None]
    row_ids = jnp.arange(rows)[:, None, None, None]
    col_ids = jnp.arange(rows)[None, None, None, :]
    identity = ((slots == 1) & (halves == side) & (row_ids == col_ids)).astype(jnp.float32)
    half_win = half_factors.reshape(rows, 3, rows)
    factor = half_win[:, :, None, :] * own_side[None, None, :, None]
    near_half = neighbours(half_factors).reshape(2, 3, rows, 3, rows)
    near_factor = near_half[:, :, :, :, None, :] * eye_side[:, None, None, None, :, None]
    for step in range(ITERS):
        if step > 0:
            near_factor = neighbours(factor.reshape(rows, 6 * rows)).reshape(2, 3, rows, 3, 2, rows)
        image = window_product(intersect_win, near_factor)
        near_image = neighbours(image.reshape(rows, 6 * rows)).reshape(2, 3, rows, 3, 2, rows)
        delta = identity - window_cross(near_factor, near_image, side)
        near_delta = neighbours(delta.reshape(rows, 6 * rows)).reshape(2, 3, rows, 3, 2, rows)
        first = window_product(factor, near_delta)
        second = window_product(first, near_delta)
        factor = keep * (factor + 0.5 * first + 0.375 * second)
    return factor.reshape(rows, 6 * rows)


def solution(mesh):
    return jax.shard_map(
        per_device,
        mesh=mesh,
        in_specs=(
            P(("pair", "side", "blk"), None),
            P(("pair", "side", "blk"), None),
            P(("pair", "side", "blk"), None),
        ),
        out_specs=P(("pair", "side", "blk"), None),
        check_vma=False,
    )
```

profile of v0, /device:TPU:0, one launch (start us, length us, event | category | flops | bytes accessed | tf_op | source)
XLA Modules:
  0.0 134.9 jit_solution(8371497596822709502)
XLA Ops:
  0.0 1.1 copy.35
  1.1 1.3 collective-permute-start.1
  2.4 5.6 %collective-permute-start = (f32[1,128,384]{1,2,0:T(8,128)S(1)}, f32[1,128,384]{1,2,0:T(8,128)S(1)}, u32[]{:S(2)}, u32[]{:S(2)}) collective-permute-start(f32[1,128,384]{1,2,0:T(8,128)S(1)} %bitcast.699), channel_id=1, source_target_pairs={{0,1},{1,2},{2,3},{4,5},{5,6},{6,7},{8,9},{9,10},{10,11},{12,13},{... | collective-permute-start | bytes 589832 | tf_op jit(solution)/shard_map/ppermute | solution.py:17
  8.0 2.9 %collective-permute-done.1 = f32[1,128,384]{1,2,0:T(8,128)S(1)} collective-permute-done((f32[1,128,384]{1,2,0:T(8,128)S(1)}, f32[1,128,384]{1,2,0:T(8,128)S(1)}, u32[]{:S(2)}, u32[]{:S(2)}) %collective-permute-start.1) | collective-permute-done | bytes 196640 | tf_op jit(solution)/shard_map/ppermute | solution.py:19
  11.0 1.2 collective-permute-done
  12.5 1.8 %collective-permute-done.2 = f32[3,128,384]{1,2,0:T(8,128)S(1)} collective-permute-done((f32[3,128,384]{1,2,0:T(8,128)S(1)}, f32[3,128,384]{1,2,0:T(8,128)S(1)}, u32[]{:S(2)}, u32[]{:S(2)}) %collective-permute-start.2) | collective-permute-done | bytes 589856 | tf_op jit(solution)/shard_map/ppermute | solution.py:33
  17.4 1.3 collective-permute-start.4
  18.7 5.0 %collective-permute-start.3 = (f32[1,128,768]{1,2,0:T(8,128)S(1)}, f32[1,128,768]{1,2,0:T(8,128)S(1)}, u32[]{:S(2)}, u32[]{:S(2)}) collective-permute-start(f32[1,128,768]{1,2,0:T(8,128)S(1)} %bitcast.710), channel_id=1, source_target_pairs={{0,1},{1,2},{2,3},{4,5},{5,6},{6,7},{8,9},{9,10},{10,11},{12,13},{... | collective-permute-start | bytes 1179656 | tf_op jit(solution)/shard_map/ppermute | solution.py:17
  23.8 7.5 %collective-permute-done.4 = f32[1,128,768]{1,2,0:T(8,128)S(1)} collective-permute-done((f32[1,128,768]{1,2,0:T(8,128)S(1)}, f32[1,128,768]{1,2,0:T(8,128)S(1)}, u32[]{:S(2)}, u32[]{:S(2)}) %collective-permute-start.4) | collective-permute-done | bytes 393248 | tf_op jit(solution)/shard_map/ppermute | solution.py:19
  31.2 1.2 collective-permute-done.3
  32.4 1.1 pad_maximum_fusion
  33.6 0.6 broadcast.201
  34.1 0.6 reduce.3
  35.2 1.6 %collective-permute-done.5 = f32[3,128,768]{1,2,0:T(8,128)} collective-permute-done((f32[3,128,768]{1,2,0:T(8,128)}, f32[3,128,768]{1,2,0:T(8,128)}, u32[]{:S(2)}, u32[]{:S(2)}) %collective-permute-start.5) | collective-permute-done | bytes 1179680 | tf_op jit(solution)/shard_map/ppermute | solution.py:33
  36.8 1.5 %broadcast_select_fusion.9 = (f32[3,128,768]{1,2,0:T(8,128)S(1)}, f32[3,128,768]{1,2,0:T(8,128)S(1)}) fusion(f32[3,128,768]{1,2,0:T(8,128)} %collective-permute-done.5, pred[]{:T(512)S(6)} %eq.69, f32[1,128,768]{1,2,0:T(8,128)S(1)} %copy-done.1, f32[1,128,768]{1,2,0:T(8,128)S(1)} %bitcast.712, f32[1,128,768]{1,2,0:T(8,128)S(1)} %copy-done.3), kind=kLoop, calls=%fused_computation.123 | loop fusion | flops 1179648 | bytes 4718593 | tf_op jit(solution)/shard_map/jit(_where)/select_n | solution.py:44
  41.2 1.3 collective-permute-start.7
  42.5 5.2 %collective-permute-start.6 = (f32[1,128,768]{1,2,0:T(8,128)S(1)}, f32[1,128,768]{1,2,0:T(8,128)S(1)}, u32[]{:S(2)}, u32[]{:S(2)}) collective-permute-start(f32[1,128,768]{1,2,0:T(8,128)S(1)} %convert_subtract_fusion.1), channel_id=1, source_target_pairs={{0,1},{1,2},{2,3},{4,5},{5,6},{6,7},{8,9},{9,10},{10,11},{12,13},{... | collective-permute-start | bytes 1179656 | tf_op jit(solution)/shard_map/ppermute | solution.py:17
  47.8 7.3 %collective-permute-done.7 = f32[1,128,768]{1,2,0:T(8,128)S(1)} collective-permute-done((f32[1,128,768]{1,2,0:T(8,128)S(1)}, f32[1,128,768]{1,2,0:T(8,128)S(1)}, u32[]{:S(2)}, u32[]{:S(2)}) %collective-permute-start.7) | collective-permute-done | bytes 393248 | tf_op jit(solution)/shard_map/ppermute | solution.py:19
  55.0 1.2 collective-permute-done.6
  56.2 1.1 pad_maximum_fusion.1
  57.7 2.7 %collective-permute-done.8 = f32[3,128,768]{1,2,0:T(8,128)S(1)} collective-permute-done((f32[3,128,768]{1,2,0:T(8,128)}, f32[3,128,768]{1,2,0:T(8,128)S(1)}, u32[]{:S(2)}, u32[]{:S(2)}) %collective-permute-start.8) | collective-permute-done | bytes 1179680 | tf_op jit(solution)/shard_map/ppermute | solution.py:33
  60.7 0.4 convolution_bitcast_fusion.37
  61.5 0.4 fusion.16
  62.7 0.4 convolution_bitcast_fusion.40
  63.9 0.4 convolution_bitcast_fusion.28
  65.2 0.4 fusion.14
  66.0 0.4 fusion.22
  67.2 1.3 collective-permute-start.10
  68.5 5.0 %collective-permute-start.9 = (f32[1,128,768]{1,2,0:T(8,128)S(1)}, f32[1,128,768]{1,2,0:T(8,128)S(1)}, u32[]{:S(2)}, u32[]{:S(2)}) collective-permute-start(f32[1,128,768]{1,2,0:T(8,128)S(1)} %add_multiply_fusion), channel_id=1, source_target_pairs={{0,1},{1,2},{2,3},{4,5},{5,6},{6,7},{8,9},{9,10},{10,11},{12,13},{... | collective-permute-start | bytes 1179656 | tf_op jit(solution)/shard_map/ppermute | solution.py:17
  73.5 7.4 %collective-permute-done.10 = f32[1,128,768]{1,2,0:T(8,128)S(1)} collective-permute-done((f32[1,128,768]{1,2,0:T(8,128)S(1)}, f32[1,128,768]{1,2,0:T(8,128)S(1)}, u32[]{:S(2)}, u32[]{:S(2)}) %collective-permute-start.10) | collective-permute-done | bytes 393248 | tf_op jit(solution)/shard_map/ppermute | solution.py:19
  81.0 1.2 collective-permute-done.9
  82.3 2.8 %collective-permute-done.11 = f32[3,128,768]{1,2,0:T(8,128)S(1)} collective-permute-done((f32[3,128,768]{1,2,0:T(8,128)S(1)}, f32[3,128,768]{1,2,0:T(8,128)S(1)}, u32[]{:S(2)}, u32[]{:S(2)}) %collective-permute-start.11) | collective-permute-done | bytes 1179680 | tf_op jit(solution)/shard_map/ppermute | solution.py:33
  88.2 1.3 collective-permute-start.13
  89.5 5.0 %collective-permute-start.12 = (f32[1,128,768]{1,2,0:T(8,128)S(1)}, f32[1,128,768]{1,2,0:T(8,128)S(1)}, u32[]{:S(2)}, u32[]{:S(2)}) collective-permute-start(f32[1,128,768]{1,2,0:T(8,128)S(1)} %bitcast.714), channel_id=1, source_target_pairs={{0,1},{1,2},{2,3},{4,5},{5,6},{6,7},{8,9},{9,10},{10,11},{12,13},{... | collective-permute-start | bytes 1179656 | tf_op jit(solution)/shard_map/ppermute | solution.py:17
  94.5 7.5 %collective-permute-done.13 = f32[1,128,768]{1,2,0:T(8,128)S(1)} collective-permute-done((f32[1,128,768]{1,2,0:T(8,128)S(1)}, f32[1,128,768]{1,2,0:T(8,128)S(1)}, u32[]{:S(2)}, u32[]{:S(2)}) %collective-permute-start.13) | collective-permute-done | bytes 393248 | tf_op jit(solution)/shard_map/ppermute | solution.py:19
  102.0 1.2 collective-permute-done.12
  103.3 2.8 %collective-permute-done.14 = f32[3,128,768]{1,2,0:T(8,128)S(1)} collective-permute-done((f32[3,128,768]{1,2,0:T(8,128)S(1)}, f32[3,128,768]{1,2,0:T(8,128)S(1)}, u32[]{:S(2)}, u32[]{:S(2)}) %collective-permute-start.14) | collective-permute-done | bytes 1179680 | tf_op jit(solution)/shard_map/ppermute | solution.py:33
  109.3 1.3 collective-permute-start.16
  110.6 5.3 %collective-permute-start.15 = (f32[1,128,768]{1,2,0:T(8,128)S(1)}, f32[1,128,768]{1,2,0:T(8,128)S(1)}, u32[]{:S(2)}, u32[]{:S(2)}) collective-permute-start(f32[1,128,768]{1,2,0:T(8,128)S(1)} %convert_subtract_fusion), channel_id=1, source_target_pairs={{0,1},{1,2},{2,3},{4,5},{5,6},{6,7},{8,9},{9,10},{10,11},{12,13},{... | collective-permute-start | bytes 1179656 | tf_op jit(solution)/shard_map/ppermute | solution.py:17
  115.8 7.2 %collective-permute-done.16 = f32[1,128,768]{1,2,0:T(8,128)S(1)} collective-permute-done((f32[1,128,768]{1,2,0:T(8,128)S(1)}, f32[1,128,768]{1,2,0:T(8,128)S(1)}, u32[]{:S(2)}, u32[]{:S(2)}) %collective-permute-start.16) | collective-permute-done | bytes 393248 | tf_op jit(solution)/shard_map/ppermute | solution.py:19
  123.1 1.2 collective-permute-done.15
  124.4 2.8 %collective-permute-done.17 = f32[3,128,768]{1,2,0:T(8,128)S(1)} collective-permute-done((f32[3,128,768]{1,2,0:T(8,128)S(1)}, f32[3,128,768]{1,2,0:T(8,128)S(1)}, u32[]{:S(2)}, u32[]{:S(2)}) %collective-permute-start.17) | collective-permute-done | bytes 1179680 | tf_op jit(solution)/shard_map/ppermute | solution.py:33
  128.4 0.4 fusion.41
  130.4 0.4 fusion.42
  131.2 0.4 convolution_bitcast_fusion.2
  132.1 0.4 fusion.39
  132.9 0.4 fusion.47
  134.0 0.9 copy.85
  (111 shorter events, 22.3 us)
Async XLA Ops:
  0.0 12.3 %copy-start.4 = (f32[128,768]{1,0:T(8,128)S(1)}, f32[128,768]{1,0:T(8,128)}, u32[]{:S(2)}) copy-start(f32[128,768]{1,0:T(8,128)} %param.3) | copy-start | bytes 1179652
  1.1 9.9 %collective-permute-start.1 = (f32[1,128,384]{1,2,0:T(8,128)S(1)}, f32[1,128,384]{1,2,0:T(8,128)S(1)}, u32[]{:S(2)}, u32[]{:S(2)}) collective-permute-start(f32[1,128,384]{1,2,0:T(8,128)S(1)} %bitcast.698), channel_id=1, source_target_pairs={{1,0},{2,1},{3,2},{5,4},{6,5},{7,6},{9,8},{10,9},{11,10},{13,12},{... | collective-permute-start | bytes 589832 | tf_op jit(solution)/shard_map/ppermute | solution.py:19
  2.4 9.7 %collective-permute-start = (f32[1,128,384]{1,2,0:T(8,128)S(1)}, f32[1,128,384]{1,2,0:T(8,128)S(1)}, u32[]{:S(2)}, u32[]{:S(2)}) collective-permute-start(f32[1,128,384]{1,2,0:T(8,128)S(1)} %bitcast.699), channel_id=1, source_target_pairs={{0,1},{1,2},{2,3},{4,5},{5,6},{6,7},{8,9},{9,10},{10,11},{12,13},{... | collective-permute-start | bytes 589832 | tf_op jit(solution)/shard_map/ppermute | solution.py:17
  12.2 2.1 %collective-permute-start.2 = (f32[3,128,384]{1,2,0:T(8,128)S(1)}, f32[3,128,384]{1,2,0:T(8,128)S(1)}, u32[]{:S(2)}, u32[]{:S(2)}) collective-permute-start(f32[3,128,384]{1,2,0:T(8,128)S(1)} %pad_maximum_fusion.5), channel_id=1, source_target_pairs={{0,4},{4,0},{1,5},{5,1},{2,6},{6,2},{3,7},{7,3},{8,12},{12,8},{9,1... | collective-permute-start | bytes 1769480 | tf_op jit(solution)/shard_map/ppermute | solution.py:33
  17.4 16.7 %copy-start.5 = (s32[1,6]{1,0:T(1,128)S(1)}, s32[1,6]{1,0:T(1,128)}, u32[]{:S(2)}) copy-start(s32[1,6]{1,0:T(1,128)} %param.5) | copy-start | bytes 76
  17.4 13.8 %collective-permute-start.4 = (f32[1,128,768]{1,2,0:T(8,128)S(1)}, f32[1,128,768]{1,2,0:T(8,128)S(1)}, u32[]{:S(2)}, u32[]{:S(2)}) collective-permute-start(f32[1,128,768]{1,2,0:T(8,128)S(1)} %bitcast.709), channel_id=1, source_target_pairs={{1,0},{2,1},{3,2},{5,4},{6,5},{7,6},{9,8},{10,9},{11,10},{13,12},{... | collective-permute-start | bytes 1179656 | tf_op jit(solution)/shard_map/ppermute | solution.py:19
  18.7 13.7 %collective-permute-start.3 = (f32[1,128,768]{1,2,0:T(8,128)S(1)}, f32[1,128,768]{1,2,0:T(8,128)S(1)}, u32[]{:S(2)}, u32[]{:S(2)}) collective-permute-start(f32[1,128,768]{1,2,0:T(8,128)S(1)} %bitcast.710), channel_id=1, source_target_pairs={{0,1},{1,2},{2,3},{4,5},{5,6},{6,7},{8,9},{9,10},{10,11},{12,13},{... | collective-permute-start | bytes 1179656 | tf_op jit(solution)/shard_map/ppermute | solution.py:17
  31.2 2.3 %copy-start = (f32[1,128,768]{1,2,0:T(8,128)}, f32[1,128,768]{1,2,0:T(8,128)S(1)}, u32[]{:S(2)}) copy-start(f32[1,128,768]{1,2,0:T(8,128)S(1)} %collective-permute-done.4) | copy-start | bytes 1179652
  32.4 1.2 copy-start.2
  33.6 3.2 %collective-permute-start.5 = (f32[3,128,768]{1,2,0:T(8,128)}, f32[3,128,768]{1,2,0:T(8,128)}, u32[]{:S(2)}, u32[]{:S(2)}) collective-permute-start(f32[3,128,768]{1,2,0:T(8,128)} %pad_maximum_fusion), channel_id=1, source_target_pairs={{0,4},{4,0},{1,5},{5,1},{2,6},{6,2},{3,7},{7,3},{8,12},{12,8},{9,1... | collective-permute-start | bytes 3538952 | tf_op jit(solution)/shard_map/ppermute | solution.py:33
  35.1 1.7 %copy-start.1 = (f32[1,128,768]{1,2,0:T(8,128)S(1)}, f32[1,128,768]{1,2,0:T(8,128)}, u32[]{:S(2)}) copy-start(f32[1,128,768]{1,2,0:T(8,128)} %copy-done) | copy-start | bytes 1179652
  35.1 1.7 %copy-start.3 = (f32[1,128,768]{1,2,0:T(8,128)S(1)}, f32[1,128,768]{1,2,0:T(8,128)}, u32[]{:S(2)}) copy-start(f32[1,128,768]{1,2,0:T(8,128)} %copy-done.2) | copy-start | bytes 1179652
  41.2 13.8 %collective-permute-start.7 = (f32[1,128,768]{1,2,0:T(8,128)S(1)}, f32[1,128,768]{1,2,0:T(8,128)S(1)}, u32[]{:S(2)}, u32[]{:S(2)}) collective-permute-start(f32[1,128,768]{1,2,0:T(8,128)S(1)} %convert_subtract_fusion.1), channel_id=1, source_target_pairs={{1,0},{2,1},{3,2},{5,4},{6,5},{7,6},{9,8},{10,9},{11,10},{13,12},{... | collective-permute-start | bytes 1179656 | tf_op jit(solution)/shard_map/ppermute | solution.py:19
  42.5 13.7 %collective-permute-start.6 = (f32[1,128,768]{1,2,0:T(8,128)S(1)}, f32[1,128,768]{1,2,0:T(8,128)S(1)}, u32[]{:S(2)}, u32[]{:S(2)}) collective-permute-start(f32[1,128,768]{1,2,0:T(8,128)S(1)} %convert_subtract_fusion.1), channel_id=1, source_target_pairs={{0,1},{1,2},{2,3},{4,5},{5,6},{6,7},{8,9},{9,10},{10,11},{12,13},{... | collective-permute-start | bytes 1179656 | tf_op jit(solution)/shard_map/ppermute | solution.py:17
  57.3 3.1 %collective-permute-start.8 = (f32[3,128,768]{1,2,0:T(8,128)}, f32[3,128,768]{1,2,0:T(8,128)S(1)}, u32[]{:S(2)}, u32[]{:S(2)}) collective-permute-start(f32[3,128,768]{1,2,0:T(8,128)} %pad_maximum_fusion.1), channel_id=1, source_target_pairs={{0,4},{4,0},{1,5},{5,1},{2,6},{6,2},{3,7},{7,3},{8,12},{12,8},{9,1... | collective-permute-start | bytes 3538952 | tf_op jit(solution)/shard_map/ppermute | solution.py:33
  67.2 13.8 %collective-permute-start.10 = (f32[1,128,768]{1,2,0:T(8,128)S(1)}, f32[1,128,768]{1,2,0:T(8,128)S(1)}, u32[]{:S(2)}, u32[]{:S(2)}) collective-permute-start(f32[1,128,768]{1,2,0:T(8,128)S(1)} %add_multiply_fusion), channel_id=1, source_target_pairs={{1,0},{2,1},{3,2},{5,4},{6,5},{7,6},{9,8},{10,9},{11,10},{13,12},{... | collective-permute-start | bytes 1179656 | tf_op jit(solution)/shard_map/ppermute | solution.py:19
  68.5 13.7 %collective-permute-start.9 = (f32[1,128,768]{1,2,0:T(8,128)S(1)}, f32[1,128,768]{1,2,0:T(8,128)S(1)}, u32[]{:S(2)}, u32[]{:S(2)}) collective-permute-start(f32[1,128,768]{1,2,0:T(8,128)S(1)} %add_multiply_fusion), channel_id=1, source_target_pairs={{0,1},{1,2},{2,3},{4,5},{5,6},{6,7},{8,9},{9,10},{10,11},{12,13},{... | collective-permute-start | bytes 1179656 | tf_op jit(solution)/shard_map/ppermute | solution.py:17
  82.2 2.9 %collective-permute-start.11 = (f32[3,128,768]{1,2,0:T(8,128)S(1)}, f32[3,128,768]{1,2,0:T(8,128)S(1)}, u32[]{:S(2)}, u32[]{:S(2)}) collective-permute-start(f32[3,128,768]{1,2,0:T(8,128)S(1)} %pad_maximum_fusion.2), channel_id=1, source_target_pairs={{0,4},{4,0},{1,5},{5,1},{2,6},{6,2},{3,7},{7,3},{8,12},{12,8},{9,1... | collective-permute-start | bytes 3538952 | tf_op jit(solution)/shard_map/ppermute | solution.py:33
  88.2 13.8 %collective-permute-start.13 = (f32[1,128,768]{1,2,0:T(8,128)S(1)}, f32[1,128,768]{1,2,0:T(8,128)S(1)}, u32[]{:S(2)}, u32[]{:S(2)}) collective-permute-start(f32[1,128,768]{1,2,0:T(8,128)S(1)} %bitcast.713), channel_id=1, source_target_pairs={{1,0},{2,1},{3,2},{5,4},{6,5},{7,6},{9,8},{10,9},{11,10},{13,12},{... | collective-permute-start | bytes 1179656 | tf_op jit(solution)/shard_map/ppermute | solution.py:19
  89.5 13.7 %collective-permute-start.12 = (f32[1,128,768]{1,2,0:T(8,128)S(1)}, f32[1,128,768]{1,2,0:T(8,128)S(1)}, u32[]{:S(2)}, u32[]{:S(2)}) collective-permute-start(f32[1,128,768]{1,2,0:T(8,128)S(1)} %bitcast.714), channel_id=1, source_target_pairs={{0,1},{1,2},{2,3},{4,5},{5,6},{6,7},{8,9},{9,10},{10,11},{12,13},{... | collective-permute-start | bytes 1179656 | tf_op jit(solution)/shard_map/ppermute | solution.py:17
  103.2 2.9 %collective-permute-start.14 = (f32[3,128,768]{1,2,0:T(8,128)S(1)}, f32[3,128,768]{1,2,0:T(8,128)S(1)}, u32[]{:S(2)}, u32[]{:S(2)}) collective-permute-start(f32[3,128,768]{1,2,0:T(8,128)S(1)} %pad_maximum_fusion.3), channel_id=1, source_target_pairs={{0,4},{4,0},{1,5},{5,1},{2,6},{6,2},{3,7},{7,3},{8,12},{12,8},{9,1... | collective-permute-start | bytes 3538952 | tf_op jit(solution)/shard_map/ppermute | solution.py:33
  109.3 13.8 %collective-permute-start.16 = (f32[1,128,768]{1,2,0:T(8,128)S(1)}, f32[1,128,768]{1,2,0:T(8,128)S(1)}, u32[]{:S(2)}, u32[]{:S(2)}) collective-permute-start(f32[1,128,768]{1,2,0:T(8,128)S(1)} %convert_subtract_fusion), channel_id=1, source_target_pairs={{1,0},{2,1},{3,2},{5,4},{6,5},{7,6},{9,8},{10,9},{11,10},{13,12},{... | collective-permute-start | bytes 1179656 | tf_op jit(solution)/shard_map/ppermute | solution.py:19
  110.6 13.7 %collective-permute-start.15 = (f32[1,128,768]{1,2,0:T(8,128)S(1)}, f32[1,128,768]{1,2,0:T(8,128)S(1)}, u32[]{:S(2)}, u32[]{:S(2)}) collective-permute-start(f32[1,128,768]{1,2,0:T(8,128)S(1)} %convert_subtract_fusion), channel_id=1, source_target_pairs={{0,1},{1,2},{2,3},{4,5},{5,6},{6,7},{8,9},{9,10},{10,11},{12,13},{... | collective-permute-start | bytes 1179656 | tf_op jit(solution)/shard_map/ppermute | solution.py:17
  124.3 2.9 %collective-permute-start.17 = (f32[3,128,768]{1,2,0:T(8,128)S(1)}, f32[3,128,768]{1,2,0:T(8,128)S(1)}, u32[]{:S(2)}, u32[]{:S(2)}) collective-permute-start(f32[3,128,768]{1,2,0:T(8,128)S(1)} %pad_maximum_fusion.4), channel_id=1, source_target_pairs={{0,4},{4,0},{1,5},{5,1},{2,6},{6,2},{3,7},{7,3},{8,12},{12,8},{9,1... | collective-permute-start | bytes 3538952 | tf_op jit(solution)/shard_map/ppermute | solution.py:33
where the time goes:
time: 136 us; the launch traced here: 135 us
  waiting for transfers between devices  61.4 us (45%)
  starting transfers between devices  39.2 us (29%)
  matrix products  21.9 us (16%)
  other arithmetic  7.41 us (5%)
  local copies, waits for them, and re-layouts  4.11 us (3%)
    ppermute x6, waiting for transfers between devices, padded(): lax.ppermute(head, axis, [((i + 1) % count, i) for i in range(ends)])  39.8 us
    ppermute x6, starting transfers between devices, padded(): lax.ppermute(tail, axis, [(i, (i + 1) % count) for i in range(ends)])  31.2 us
    dot_general x42, matrix products, window_product(): lax.dot_general(left[:, slot], nearby[:, slot, :, source], (((1, 2), (0,...  16.5 us
    ppermute x6, waiting for transfers between devices, swapped(): return lax.ppermute(block, axis, route)  14.5 us
    ppermute x6, starting transfers between devices, padded(): lax.ppermute(head, axis, [((i + 1) % count, i) for i in range(ends)])  7.75 us
    ppermute x6, waiting for transfers between devices, padded(): lax.ppermute(tail, axis, [(i, (i + 1) % count) for i in range(ends)])  7.08 us
    dot_general x14, matrix products, window_cross(): lax.dot_general(mines[slot], near_image[:, slot, :, source], (((0, 1), (0...  5.4 us
  transfers between devices with their start and end apart: 18, of which 18 were waited for; matrix products, arithmetic and copies ran while one was open for 2% of the time, Pallas kernels for 0%

commit v1 on v0

v1 whole, which is shorter than its diff:
```python
import functools

import jax
import jax.numpy as jnp
from jax import lax
from jax.experimental import pallas as pl
from jax.experimental.pallas import tpu as pltpu
from jax.sharding import PartitionSpec as P

ITERS = 2
MESH = pl.DeviceIdType.MESH
F32 = jnp.float32
BF16 = jnp.bfloat16


def parts(x):
    high = x.astype(BF16)
    return high, (x - high.astype(F32)).astype(BF16)


def mm(a, b, ta=False):
    dims = (((0 if ta else 1,), (0,)), ((), ()))

    def dot(x, y):
        return lax.dot_general(x, y, dims, preferred_element_type=F32)

    cols = b[0].shape[1]
    if cols <= 128:
        wide = dot(a[0], jnp.concatenate(b, axis=1))
        return wide[:, :cols] + wide[:, cols:] + dot(a[1], b[0])
    if ta:
        return dot(a[0], b[0]) + dot(a[1], b[0]) + dot(a[0], b[1])
    rows = a[0].shape[0]
    tall = dot(jnp.concatenate(a, axis=0), b[0])
    return tall[:rows] + tall[rows:] + dot(a[0], b[1])


def put(ref, rows, cols, x):
    high, low = parts(x)
    ref[0, rows, cols] = high
    ref[1, rows, cols] = low


def get(ref, rows, cols):
    return ref[0, rows, cols], ref[1, rows, cols]


def cat(pairs, axis):
    return tuple(jnp.concatenate([p[i] for p in pairs], axis=axis) for i in range(2))


Z_EDGE, Z_S, Z_DIAG, Z_PAT, Z_I, Z_D, Z_F, Z_NEW = 0, 1, 2, 3, 4, 6, 8, 9
Z_COUNT = 10
X_ROW, X_EDGE, X_S, X_DIAG, X_COL, X_DD, X_DN, X_NEWN, X_NEWD, X_NEW = 0, 1, 2, 3, 4, 5, 7, 9, 10, 11
X_COUNT = 12


def kernel(
    n, s_ref, h_ref, p_ref, o_ref,
    sx, hx, edge, edge_x, snb, snb_x, diag, diag_x, pat,
    i_out, d_out, i_in, d_in, d_fw, dcol_out, dcol_in, dn_out, dn_in,
    f_out, f_in, z_out, z_in, zn_out, zn_in, zd_out, zd_in, zd_fw,
    sb, sd, zrow, zcol, znd, dcol, dn, dd,
    zs, zr, xs, xr,
):
    side = lax.axis_index("side")
    c = lax.axis_index("blk")
    R = s_ref.shape[0]
    W = 2 * R
    T = p_ref.shape[0]
    tile = R // T
    has = (c > 0, c < n - 1)
    peer = ({"blk": jnp.maximum(c - 1, 0)}, {"blk": jnp.minimum(c + 1, n - 1)})
    sib = {"side": 1 - side}
    mine = pl.ds(pl.multiple_of(side * R, R), R)
    other = pl.ds(pl.multiple_of((1 - side) * R, R), R)
    full = slice(0, W)
    blk = [slice(e * W, (e + 1) * W) for e in range(3)]
    near = (0, 2)
    sent = []

    def z_copy(m, k, src, buf):
        return pltpu.make_async_remote_copy(
            src_ref=src, dst_ref=buf.at[1 - k], send_sem=zs.at[m, k], recv_sem=zr.at[m, 1 - k],
            device_id=peer[k], device_id_type=MESH)

    def z_send(m, k, src, buf):
        copy = z_copy(m, k, src, buf)
        pl.when(has[k])(copy.start)
        sent.append((has[k], copy))

    def z_wait(m, k, buf):
        copy = pltpu.make_async_remote_copy(
            src_ref=buf.at[k], dst_ref=buf.at[k], send_sem=zs.at[m, k], recv_sem=zr.at[m, k],
            device_id=peer[k], device_id_type=MESH)
        pl.when(has[k])(copy.wait_recv)

    def x_copy(m, k, src, dst):
        return pltpu.make_async_remote_copy(
            src_ref=src, dst_ref=dst, send_sem=xs.at[m, k], recv_sem=xr.at[m, k],
            device_id=sib, device_id_type=MESH)

    def x_send(m, k, src, dst):
        copy = x_copy(m, k, src, dst)
        copy.start()
        sent.append((None, copy))

    def x_wait(m, k, dst):
        x_copy(m, k, dst, dst).wait_recv()

    def forward(m, k, buf, dst):
        copy = x_copy(m, k, buf.at[k], dst.at[k])
        pl.when(has[k])(copy.start)
        sent.append((has[k], copy))

    def forward_wait(m, k, dst):
        pl.when(has[k])(x_copy(m, k, dst.at[k], dst.at[k]).wait_recv)

    barrier = pltpu.get_barrier_semaphore()
    pl.semaphore_signal(barrier, inc=1, device_id=sib, device_id_type=MESH)
    for k in range(2):
        @pl.when(has[k])
        def _():
            pl.semaphore_signal(barrier, inc=1, device_id=peer[k], device_id_type=MESH)

    for k in range(2):
        @pl.when(jnp.logical_not(has[k]))
        def _():
            for ref in (edge, edge_x, snb, snb_x, diag, diag_x, f_in, zd_in, zd_fw, pat):
                ref[k] = jnp.zeros(ref.shape[1:], ref.dtype)
            for ref in (i_in, d_in, d_fw):
                for t in range(ITERS):
                    ref[t, k] = jnp.zeros(ref.shape[2:], ref.dtype)
    zrow[...] = jnp.zeros(zrow.shape, BF16)
    zcol[...] = jnp.zeros(zcol.shape, BF16)
    znd[...] = jnp.zeros(znd.shape, BF16)
    put(sb, mine, slice(None), s_ref[...])
    for e in range(3):
        put(zrow, mine, pl.ds(pl.multiple_of(e * W + side * R, R), R), h_ref[:, e * R:(e + 1) * R])
    pl.semaphore_wait(barrier, 1 + has[0].astype(jnp.int32) + has[1].astype(jnp.int32))

    for k in range(2):
        z_send(Z_EDGE, k, h_ref.at[:, pl.ds(near[k] * R, R)], edge)
    x_send(X_ROW, 0, h_ref, hx)
    x_send(X_ROW, 1, s_ref, sx)
    for k in range(2):
        z_send(Z_S, k, s_ref.at[:, pl.ds(W, W)], snb)
        z_send(Z_PAT, k, p_ref, pat)
    for k in range(2):
        z_send(Z_DIAG, k, h_ref.at[:, pl.ds(R, R)], diag)

    x_wait(X_ROW, 0, hx)
    for e in range(3):
        put(zrow, other, pl.ds(pl.multiple_of(e * W + (1 - side) * R, R), R), hx[:, e * R:(e + 1) * R])
    x_wait(X_ROW, 1, sx)
    put(sb, other, slice(None), sx[...])
    for i in range(2):
        zcol[i, blk[1]] = zrow[i, :, blk[1]]
    for k in range(2):
        z_wait(Z_EDGE, k, edge)
        forward(X_EDGE, k, edge, edge_x)
        rows = pl.ds(pl.multiple_of(near[k] * W + side * R, R), R)
        put(zcol, rows, mine, edge[k])
    for k in range(2):
        z_wait(Z_S, k, snb)
        forward(X_S, k, snb, snb_x)
        put(sd.at[k], mine, full, snb[k])
    for k in range(2):
        forward_wait(X_EDGE, k, edge_x)
        rows = pl.ds(pl.multiple_of(near[k] * W + (1 - side) * R, R), R)
        put(zcol, rows, other, edge_x[k])

    eye = (lax.broadcasted_iota(jnp.int32, (W, R), 0) == lax.broadcasted_iota(jnp.int32, (W, R), 1) + side * R).astype(F32)

    def kept(grid, slot, here):
        rows_out = []
        for a in range(T):
            row = []
            for g in range(2):
                for b in range(T):
                    q = (slot * 2 + g) * T + b
                    value = grid[a:a + 1, q:q + 1].astype(F32)
                    if here and slot == 1 and a == b:
                        value = jnp.maximum(value, (side == g).astype(F32))
                    row.append(jnp.broadcast_to(value, (tile, tile)))
            rows_out.append(jnp.concatenate(row, axis=1))
        return jnp.concatenate(rows_out, axis=0) if T > 1 else rows_out[0]

    def window_of_half(block):
        zero = jnp.zeros_like(block)
        return jnp.concatenate([jnp.where(side == 0, block, zero), jnp.where(side == 0, zero, block)], axis=1)

    old = [window_of_half(h_ref[:, e * R:(e + 1) * R]) for e in range(3)]
    for t in range(ITERS):
        last = t == ITERS - 1
        icc = mm(get(sb, full, slice(None)), get(zcol, slice(None), mine))
        i_out[t] = icc
        for k in range(2):
            z_send(Z_I + t, k, i_out.at[t], i_in.at[t])
        if t == 0:
            for k in range(2):
                forward_wait(X_S, k, snb_x)
                put(sd.at[k], other, full, snb_x[k])
        inear = []
        for k in range(2):
            inear.append(
                mm(get(sb, full, blk[near[k]]), get(zcol, blk[1], mine), ta=True)
                + mm(get(sd.at[k], full, full), get(zcol, blk[near[k]], mine)))
        icc = parts(icc)
        inear = [parts(x) for x in inear]
        icol = cat([inear[0], icc, inear[1]], 0)
        dcc = eye - mm(get(zcol, slice(None), full), icol, ta=True)
        d_out[t] = dcc
        for k in range(2):
            z_send(Z_D + t, k, d_out.at[t], d_in.at[t])
        if t == 0:
            for k in range(2):
                z_wait(Z_DIAG, k, diag)
                forward(X_DIAG, k, diag, diag_x)
                put(znd.at[k], mine, mine, diag[k])
            for k in range(2):
                forward_wait(X_DIAG, k, diag_x)
                put(znd.at[k], other, other, diag_x[k])
        else:
            for k in range(2):
                z_wait(Z_NEW, k, zd_in)
                forward(X_NEWD, k, zd_in, zd_fw)
                put(znd.at[k], mine, full, zd_in[k])
            for k in range(2):
                forward_wait(X_NEWD, k, zd_fw)
                put(znd.at[k], other, full, zd_fw[k])
        dcol_out[t, blk[1]] = dcc
        put(dcol, blk[1], mine, dcc)
        for k in range(2):
            dside = -(mm(get(zrow, full, blk[near[k]]), icc, ta=True) + mm(get(znd.at[k], full, full), inear[k], ta=True))
            dcol_out[t, blk[near[k]]] = dside
            put(dcol, blk[near[k]], mine, dside)
        x_send(X_COL, t, dcol_out.at[t], dcol_in.at[t])
        iside = []
        for k in range(2):
            iside.append(parts(
                mm(get(sb, full, blk[1]), get(zrow, full, pl.ds(pl.multiple_of(near[k] * W + side * R, R), R)))
                + mm(get(sb, full, blk[near[k]]), get(znd.at[k], full, mine))))
        dpart = [mm(get(zrow, full, blk[1]), iside[k], ta=True) for k in range(2)]
        x_wait(X_COL, t, dcol_in.at[t])
        put(dcol, slice(None), other, dcol_in[t])
        fcc = mm(get(zrow, mine, slice(None)), get(dcol, slice(None), full))
        if not last:
            f_out[...] = fcc
            for k in range(2):
                z_send(Z_F, k, f_out, f_in)
            fnear = []
            for k in range(2):
                rows = pl.ds(pl.multiple_of(near[k] * W + side * R, R), R)
                fnear.append(
                    mm(get(zcol, rows, full), get(dcol, blk[1], full))
                    + mm(get(znd.at[k], mine, full), get(dcol, blk[near[k]], full)))
        for k in range(2):
            z_wait(Z_I + t, k, i_in.at[t])
            value = -(dpart[k] + mm(get(zcol, blk[near[k]], full), parts(i_in[t, k]), ta=True))
            dn_out[t, k] = value
            x_send(X_DN + t, k, dn_out.at[t, k], dn_in.at[t, k])
            put(dn.at[k], full, mine, value)
        for k in range(2):
            z_wait(Z_D + t, k, d_in.at[t])
            forward(X_DD + t, k, d_in.at[t], d_fw.at[t])
            put(dd.at[k], full, mine, d_in[t, k])
        for k in range(2):
            x_wait(X_DN + t, k, dn_in.at[t, k])
            put(dn.at[k], full, other, dn_in[t, k])
        for k in range(2):
            forward_wait(X_DD + t, k, d_fw.at[t])
            put(dd.at[k], full, other, d_fw[t, k])
        fside = [
            mm(get(zrow, mine, blk[1]), get(dn.at[k], full, full)) + mm(get(zrow, mine, blk[near[k]]), get(dd.at[k], full, full))
            for k in range(2)
        ]
        fc = parts(fcc)
        fs = [parts(x) for x in fside]
        gcc = mm(cat([fs[0], fc, fs[1]], 1), get(dcol, slice(None), full))
        own = p_ref[...]
        new = [None, None, None]
        new[1] = kept(own, 1, True) * (old[1] + 0.5 * fcc + 0.375 * gcc)
        if not last:
            zd_out[...] = new[1]
            for k in range(2):
                z_send(Z_NEW, k, zd_out, zd_in)
            for k in range(2):
                z_wait(Z_F, k, f_in)
                gnear = mm(parts(fnear[k]), get(dcol, blk[1], full)) + mm(parts(f_in[k]), get(dcol, blk[near[k]], full))
                if True:
                    z_wait(Z_PAT, k, pat)
                    mask = kept(pat.at[k][...], near[1 - k], False)
                zn = mask * (window_of_half(edge[k]) + 0.5 * fnear[k] + 0.375 * gnear)
                zn_out[k] = zn
                x_send(X_NEWN, k, zn_out.at[k], zn_in.at[k])
                rows = pl.ds(pl.multiple_of(near[k] * W + side * R, R), R)
                put(zcol, rows, full, zn)
        for k in range(2):
            e = near[k]
            gside = mm(fc, get(dn.at[k], full, full)) + mm(fs[k], get(dd.at[k], full, full))
            new[e] = kept(own, e, True) * (old[e] + 0.5 * fside[k] + 0.375 * gside)
        if last:
            for e in range(3):
                o_ref[:, blk[e]] = new[e]
        else:
            for e in range(3):
                z_out[:, blk[e]] = new[e]
            x_send(X_NEW, 0, z_out, z_in)
            for e in range(3):
                put(zrow, mine, blk[e], new[e])
            for k in range(2):
                x_wait(X_NEWN, k, zn_in.at[k])
                rows = pl.ds(pl.multiple_of(near[k] * W + (1 - side) * R, R), R)
                put(zcol, rows, full, zn_in[k])
            x_wait(X_NEW, 0, z_in)
            put(zrow, other, slice(None), z_in[...])
            for i in range(2):
                zcol[i, blk[1]] = zrow[i, :, blk[1]]
            old = new

    for cond, copy in sent:
        if cond is None:
            copy.wait_send()
        else:
            pl.when(cond)(copy.wait_send)


def solution(mesh):
    n = mesh.shape["blk"]

    def per_device(intersect, half_factors, z_pattern):
        R = intersect.shape[0]
        W = 2 * R

        def f32(*shape):
            return pltpu.VMEM(shape, F32)

        def b16(*shape):
            return pltpu.VMEM(shape, BF16)

        return pl.pallas_call(
            functools.partial(kernel, n),
            out_shape=jax.ShapeDtypeStruct(intersect.shape, F32),
            in_specs=[pl.BlockSpec(memory_space=pltpu.VMEM)] * 3,
            out_specs=pl.BlockSpec(memory_space=pltpu.VMEM),
            scratch_shapes=[
                f32(R, 3 * W), f32(R, 3 * R), f32(2, R, R), f32(2, R, R), f32(2, R, W), f32(2, R, W),
                f32(2, R, R), f32(2, R, R), pltpu.VMEM((2,) + z_pattern.shape, z_pattern.dtype),
                f32(ITERS, W, R), f32(ITERS, W, R), f32(ITERS, 2, W, R), f32(ITERS, 2, W, R), f32(ITERS, 2, W, R),
                f32(ITERS, 3 * W, R), f32(ITERS, 3 * W, R), f32(ITERS, 2, W, R), f32(ITERS, 2, W, R),
                f32(R, W), f32(2, R, W), f32(R, 3 * W), f32(R, 3 * W), f32(2, R, W), f32(2, R, W),
                f32(R, W), f32(2, R, W), f32(2, R, W),
                b16(2, W, 3 * W), b16(2, 2, W, W), b16(2, W, 3 * W), b16(2, 3 * W, W), b16(2, 2, W, W),
                b16(2, 3 * W, W), b16(2, 2, W, W), b16(2, 2, W, W),
                pltpu.SemaphoreType.DMA((Z_COUNT, 2)), pltpu.SemaphoreType.DMA((Z_COUNT, 2)),
                pltpu.SemaphoreType.DMA((X_COUNT, 2)), pltpu.SemaphoreType.DMA((X_COUNT, 2)),
            ],
            compiler_params=pltpu.CompilerParams(collective_id=0, has_side_effects=True),
        )(intersect, half_factors, z_pattern)

    return jax.shard_map(
        per_device,
        mesh=mesh,
        in_specs=(
            P(("pair", "side", "blk"), None),
            P(("pair", "side", "blk"), None),
            P(("pair", "side", "blk"), None),
        ),
        out_specs=P(("pair", "side", "blk"), None),
        check_vma=False,
    )
```

time: 136 us -> 37.1 us (0.27)
  waiting for transfers between devices: 61.4 us -> 0 us
  starting transfers between devices: 39.2 us -> 0 us
  Pallas kernels: 0 us -> 34.8 us
  matrix products: 21.9 us -> 0 us
  other arithmetic: 7.41 us -> 0 us
  local copies, waits for them, and re-layouts: 4.11 us -> 1.77 us
    ppermute x18 -> x0, waiting for transfers between devices: 61.4 us -> none  [the longest x6 39.8 us: padded(): lax.ppermute(head, axis, [((i + 1) % count, i) for i in range(ends)])]
    ppermute x18 -> x0, starting transfers between devices: 39.2 us -> none  [the longest x6 31.2 us: padded(): lax.ppermute(tail, axis, [(i, (i + 1) % count) for i in range(ends)])]
    pallas_call x0 -> x1, Pallas kernels: none -> 34.8 us  [per_device(): pl.pallas_call(functools.partial(kernel, n), out_shape=jax.ShapeDtypeStru...]
    dot_general x56 -> x0, matrix products: 21.9 us -> none  [the longest x42 16.5 us: window_product(): lax.dot_general(left[:, slot], nearby[:, slot, :, source], (((1, 2), (0,...]
    concatenate x6 -> x0, other arithmetic: 2.55 us -> none  [padded(): jnp.concatenate([lax.ppermute(tail, axis, [(i, (i + 1) % count) for i in...]
    select_n x6 -> x0, other arithmetic: 2.2 us -> none  [neighbours(): jnp.where(side == 0, local, other)]
    mul x9 -> x0, local copies, waits for them, and re-layouts: 1.8 us -> none  [the longest x5 1.57 us: per_device(): factor = keep * (factor + 0.5 * first + 0.375 * second)]
  transfers between devices with their start and end apart: 18 -> 0, of which waited for: 18 -> 0; matrix products, arithmetic and copies ran while one was open for 2% -> 0% of each run, Pallas kernels for 0% -> 0%
where the time goes in v1:
time: 37.1 us; the launch traced here: 36.6 us
  Pallas kernels  34.8 us (94%)
  local copies, waits for them, and re-layouts  1.77 us (5%)
    pallas_call x1, Pallas kernels, per_device(): pl.pallas_call(functools.partial(kernel, n), out_shape=jax.ShapeDtypeStru...  34.8 us
    unnamed x1, local copies, waits for them, and re-layouts  1.77 us

profile of v1, /device:TPU:0, one launch (start us, length us, event | category | flops | bytes accessed | tf_op | source)
XLA Modules:
  0.0 36.6 jit_solution(14039084073089072)
XLA Ops:
  0.0 34.8 %shard_map.37 = f32[128,768]{1,0:T(8,128)} custom-call(f32[128,768]{1,0:T(8,128)} %s_ref.1, f32[128,384]{1,0:T(8,128)} %h_ref.1, s32[1,6]{1,0:T(1,128)} %p_ref.1), custom_call_target="tpu_custom_call" | custom-call | tf_op jit(solution)/shard_map/pallas_call | solution.py:342
  34.9 1.8 %copy.5 = f32[128,768]{1,0:T(8,128)} copy(f32[128,768]{1,0:T(8,128)} %shard_map.37) | data formatting | bytes 786432

commit v2 on v1

--- a/solution.py
+++ b/solution.py
@@ -10,6 +10,7 @@
 ITERS = 2
 MESH = pl.DeviceIdType.MESH
 F32 = jnp.float32
+VMEM_KIB = 54200
 BF16 = jnp.bfloat16
 
 
@@ -49,6 +50,12 @@
     return tuple(jnp.concatenate([p[i] for p in pairs], axis=axis) for i in range(2))
 
 
+def half_of_upper(block):
+    split = block.shape[0] // 2
+    turned = block.T
+    return turned[:split], block[split:]
+
+
 Z_EDGE, Z_S, Z_DIAG, Z_PAT, Z_I, Z_D, Z_F, Z_NEW = 0, 1, 2, 3, 4, 6, 8, 9
 Z_COUNT = 10
 X_ROW, X_EDGE, X_S, X_DIAG, X_COL, X_DD, X_DN, X_NEWN, X_NEWD, X_NEW = 0, 1, 2, 3, 4, 5, 7, 9, 10, 11
@@ -56,12 +63,13 @@
 
 
 def kernel(
-    n, s_ref, h_ref, p_ref, o_ref,
+    n, s_hbm, h_ref, p_ref, o_ref, k_ref,
+    s_ref, s_out,
     sx, hx, edge, edge_x, snb, snb_x, diag, diag_x, pat,
     i_out, d_out, i_in, d_in, d_fw, dcol_out, dcol_in, dn_out, dn_in,
     f_out, f_in, z_out, z_in, zn_out, zn_in, zd_out, zd_in, zd_fw,
     sb, sd, zrow, zcol, znd, dcol, dn, dd,
-    zs, zr, xs, xr,
+    zs, zr, xs, xr, ls,
 ):
     side = lax.axis_index("side")
     c = lax.axis_index("blk")
@@ -123,6 +131,8 @@
         def _():
             pl.semaphore_signal(barrier, inc=1, device_id=peer[k], device_id_type=MESH)
 
+    load = pltpu.make_async_copy(s_hbm, s_ref, ls)
+    load.start()
     for k in range(2):
         @pl.when(jnp.logical_not(has[k]))
         def _():
@@ -134,21 +144,25 @@
     zrow[...] = jnp.zeros(zrow.shape, BF16)
     zcol[...] = jnp.zeros(zcol.shape, BF16)
     znd[...] = jnp.zeros(znd.shape, BF16)
+    pl.semaphore_wait(barrier, 1 + has[0].astype(jnp.int32) + has[1].astype(jnp.int32))
+
+    for k in range(2):
+        z_send(Z_EDGE, k, h_ref.at[:, pl.ds(near[k] * R, R)], edge)
+    x_send(X_ROW, 0, h_ref, hx)
+    load.wait()
+    left, right = s_ref[:, W:W + R], s_ref[:, W + R:2 * W]
+    s_out[:R] = jnp.where(side == 0, left, right)
+    s_out[R:] = jnp.where(side == 0, right[:R // 2], left.T[R // 2:])
+    for k in range(2):
+        z_send(Z_S, k, s_out, snb)
+        z_send(Z_PAT, k, p_ref, pat)
+    x_send(X_ROW, 1, s_ref, sx)
+    for k in range(2):
+        z_send(Z_DIAG, k, h_ref.at[:, pl.ds(R, R)], diag)
+
     put(sb, mine, slice(None), s_ref[...])
     for e in range(3):
         put(zrow, mine, pl.ds(pl.multiple_of(e * W + side * R, R), R), h_ref[:, e * R:(e + 1) * R])
-    pl.semaphore_wait(barrier, 1 + has[0].astype(jnp.int32) + has[1].astype(jnp.int32))
-
-    for k in range(2):
-        z_send(Z_EDGE, k, h_ref.at[:, pl.ds(near[k] * R, R)], edge)
-    x_send(X_ROW, 0, h_ref, hx)
-    x_send(X_ROW, 1, s_ref, sx)
-    for k in range(2):
-        z_send(Z_S, k, s_ref.at[:, pl.ds(W, W)], snb)
-        z_send(Z_PAT, k, p_ref, pat)
-    for k in range(2):
-        z_send(Z_DIAG, k, h_ref.at[:, pl.ds(R, R)], diag)
-
     x_wait(X_ROW, 0, hx)
     for e in range(3):
         put(zrow, other, pl.ds(pl.multiple_of(e * W + (1 - side) * R, R), R), hx[:, e * R:(e + 1) * R])
@@ -164,7 +178,7 @@
     for k in range(2):
         z_wait(Z_S, k, snb)
         forward(X_S, k, snb, snb_x)
-        put(sd.at[k], mine, full, snb[k])
+        put(sd.at[k], mine, mine, snb[k, :R])
     for k in range(2):
         forward_wait(X_EDGE, k, edge_x)
         rows = pl.ds(pl.multiple_of(near[k] * W + (1 - side) * R, R), R)
@@ -186,6 +200,21 @@
             rows_out.append(jnp.concatenate(row, axis=1))
         return jnp.concatenate(rows_out, axis=0) if T > 1 else rows_out[0]
 
+    for a in range(T):
+        for slot in range(3):
+            for g in range(2):
+                for b in range(T):
+                    q = (slot * 2 + g) * T + b
+                    value = p_ref[a:a + 1, q:q + 1].astype(F32)
+                    if slot == 1 and a == b:
+                        value = jnp.maximum(value, (side == g).astype(F32))
+                    k_ref[a * tile:(a + 1) * tile, q * tile:(q + 1) * tile] = jnp.broadcast_to(value, (tile, tile))
+
+    def put_pair(ref, here, there):
+        upper = jnp.concatenate([jnp.where(side == 0, here, there), jnp.where(side == 0, there, here)], axis=0)
+        put(ref, slice(0, R), slice(R, W), upper)
+        put(ref, slice(R, W), slice(0, R), upper.T)
+
     def window_of_half(block):
         zero = jnp.zeros_like(block)
         return jnp.concatenate([jnp.where(side == 0, block, zero), jnp.where(side == 0, zero, block)], axis=1)
@@ -200,7 +229,8 @@
         if t == 0:
             for k in range(2):
                 forward_wait(X_S, k, snb_x)
-                put(sd.at[k], other, full, snb_x[k])
+                put(sd.at[k], other, other, snb_x[k, :R])
+                put_pair(sd.at[k], snb[k, R:], snb_x[k, R:])
         inear = []
         for k in range(2):
             inear.append(
@@ -210,7 +240,11 @@
         inear = [parts(x) for x in inear]
         icol = cat([inear[0], icc, inear[1]], 0)
         dcc = eye - mm(get(zcol, slice(None), full), icol, ta=True)
-        d_out[t] = dcc
+        own_tile = jnp.where(side == 0, dcc[:R], dcc[R:])
+        off_tile = jnp.where(side == 0, dcc[R:], dcc[:R])
+        first_half, second_half = half_of_upper(off_tile)
+        d_out[t, :R] = own_tile
+        d_out[t, R:] = jnp.where(side == 0, first_half, second_half)
         for k in range(2):
             z_send(Z_D + t, k, d_out.at[t], d_in.at[t])
         if t == 0:
@@ -261,26 +295,30 @@
             dn_out[t, k] = value
             x_send(X_DN + t, k, dn_out.at[t, k], dn_in.at[t, k])
             put(dn.at[k], full, mine, value)
+        fc = parts(fcc)
+        gcc = mm(fc, get(dcol, blk[1], full))
+        fhalf, ghalf = [], []
+        for k in range(2):
+            x_wait(X_DN + t, k, dn_in.at[t, k])
+            put(dn.at[k], full, other, dn_in[t, k])
+            fhalf.append(mm(get(zrow, mine, blk[1]), get(dn.at[k], full, full)))
+            ghalf.append(mm(fc, get(dn.at[k], full, full)))
         for k in range(2):
             z_wait(Z_D + t, k, d_in.at[t])
             forward(X_DD + t, k, d_in.at[t], d_fw.at[t])
-            put(dd.at[k], full, mine, d_in[t, k])
-        for k in range(2):
-            x_wait(X_DN + t, k, dn_in.at[t, k])
-            put(dn.at[k], full, other, dn_in[t, k])
-        for k in range(2):
+        for k in range(2):
+            put(dd.at[k], mine, mine, d_in[t, k, :R])
             forward_wait(X_DD + t, k, d_fw.at[t])
-            put(dd.at[k], full, other, d_fw[t, k])
-        fside = [
-            mm(get(zrow, mine, blk[1]), get(dn.at[k], full, full)) + mm(get(zrow, mine, blk[near[k]]), get(dd.at[k], full, full))
-            for k in range(2)
-        ]
-        fc = parts(fcc)
+            put(dd.at[k], other, other, d_fw[t, k, :R])
+            put_pair(dd.at[k], d_in[t, k, R:], d_fw[t, k, R:])
+        fside = [fhalf[k] + mm(get(zrow, mine, blk[near[k]]), get(dd.at[k], full, full)) for k in range(2)]
         fs = [parts(x) for x in fside]
-        gcc = mm(cat([fs[0], fc, fs[1]], 1), get(dcol, slice(None), full))
+        for k in range(2):
+            gcc = gcc + mm(fs[k], get(dcol, blk[near[k]], full))
         own = p_ref[...]
         new = [None, None, None]
-        new[1] = kept(own, 1, True) * (old[1] + 0.5 * fcc + 0.375 * gcc)
+        mask = 1.0 if last else kept(own, 1, True)
+        new[1] = mask * (old[1] + 0.5 * fcc + 0.375 * gcc)
         if not last:
             zd_out[...] = new[1]
             for k in range(2):
@@ -298,8 +336,9 @@
                 put(zcol, rows, full, zn)
         for k in range(2):
             e = near[k]
-            gside = mm(fc, get(dn.at[k], full, full)) + mm(fs[k], get(dd.at[k], full, full))
-            new[e] = kept(own, e, True) * (old[e] + 0.5 * fside[k] + 0.375 * gside)
+            gside = ghalf[k] + mm(fs[k], get(dd.at[k], full, full))
+            mask = 1.0 if last else kept(own, e, True)
+            new[e] = mask * (old[e] + 0.5 * fside[k] + 0.375 * gside)
         if last:
             for e in range(3):
                 o_ref[:, blk[e]] = new[e]
@@ -339,15 +378,16 @@
         def b16(*shape):
             return pltpu.VMEM(shape, BF16)
 
-        return pl.pallas_call(
+        refined, keep = pl.pallas_call(
             functools.partial(kernel, n),
-            out_shape=jax.ShapeDtypeStruct(intersect.shape, F32),
-            in_specs=[pl.BlockSpec(memory_space=pltpu.VMEM)] * 3,
-            out_specs=pl.BlockSpec(memory_space=pltpu.VMEM),
+            out_shape=(jax.ShapeDtypeStruct(intersect.shape, F32), jax.ShapeDtypeStruct(intersect.shape, F32)),
+            in_specs=[pl.BlockSpec(memory_space=m) for m in (pltpu.HBM, pltpu.VMEM, pltpu.VMEM)],
+            out_specs=[pl.BlockSpec(memory_space=pltpu.VMEM)] * 2,
             scratch_shapes=[
-                f32(R, 3 * W), f32(R, 3 * R), f32(2, R, R), f32(2, R, R), f32(2, R, W), f32(2, R, W),
+                f32(*intersect.shape), f32(W - R // 2, R),
+                f32(R, 3 * W), f32(R, 3 * R), f32(2, R, R), f32(2, R, R), f32(2, W - R // 2, R), f32(2, W - R // 2, R),
                 f32(2, R, R), f32(2, R, R), pltpu.VMEM((2,) + z_pattern.shape, z_pattern.dtype),
-                f32(ITERS, W, R), f32(ITERS, W, R), f32(ITERS, 2, W, R), f32(ITERS, 2, W, R), f32(ITERS, 2, W, R),
+                f32(ITERS, W, R), f32(ITERS, W - R // 2, R), f32(ITERS, 2, W, R), f32(ITERS, 2, W - R // 2, R), f32(ITERS, 2, W - R // 2, R),
                 f32(ITERS, 3 * W, R), f32(ITERS, 3 * W, R), f32(ITERS, 2, W, R), f32(ITERS, 2, W, R),
                 f32(R, W), f32(2, R, W), f32(R, 3 * W), f32(R, 3 * W), f32(2, R, W), f32(2, R, W),
                 f32(R, W), f32(2, R, W), f32(2, R, W),
@@ -355,9 +395,11 @@
                 b16(2, 3 * W, W), b16(2, 2, W, W), b16(2, 2, W, W),
                 pltpu.SemaphoreType.DMA((Z_COUNT, 2)), pltpu.SemaphoreType.DMA((Z_COUNT, 2)),
                 pltpu.SemaphoreType.DMA((X_COUNT, 2)), pltpu.SemaphoreType.DMA((X_COUNT, 2)),
+                pltpu.SemaphoreType.DMA,
             ],
-            compiler_params=pltpu.CompilerParams(collective_id=0, has_side_effects=True),
+            compiler_params=pltpu.CompilerParams(collective_id=0, has_side_effects=True, vmem_limit_bytes=VMEM_KIB * 1024),
         )(intersect, half_factors, z_pattern)
+        return keep * refined
 
     return jax.shard_map(
         per_device,

time: 37.1 us -> 34.9 us (0.941)
  Pallas kernels: 34.8 us -> 32.4 us
  other arithmetic: 0 us -> 0.79 us
    pallas_call x1, Pallas kernels: 34.8 us -> 32.4 us  [per_device(): pl.pallas_call(functools.partial(kernel, n), out_shape=(jax.ShapeDtypeStr...]
    mul x0 -> x1, other arithmetic: none -> 0.79 us  [per_device(): return keep * refined]
    unnamed x1 -> x4, local copies, waits for them, and re-layouts: 1.77 us -> 1.58 us
where the time goes in v2:
time: 34.9 us; the launch traced here: 34.8 us
  Pallas kernels  32.4 us (93%)
  local copies, waits for them, and re-layouts  1.58 us (5%)
  other arithmetic  0.79 us (2%)
    pallas_call x1, Pallas kernels, per_device(): pl.pallas_call(functools.partial(kernel, n), out_shape=(jax.ShapeDtypeStr...  32.4 us
    unnamed x4, local copies, waits for them, and re-layouts  1.58 us
    mul x1, other arithmetic, per_device(): return keep * refined  0.79 us

profile of v2, /device:TPU:0, one launch (start us, length us, event | category | flops | bytes accessed | tf_op | source)
XLA Modules:
  0.0 34.8 jit_solution(2763541190453892370)
XLA Ops:
  0.0 0.0 copy-start
  0.0 0.9 %copy-done = f32[128,384]{1,0:T(8,128)S(1)} copy-done((f32[128,384]{1,0:T(8,128)S(1)}, f32[128,384]{1,0:T(8,128)}, u32[]{:S(2)}) %copy-start) | copy-done | bytes 196632
  0.9 0.0 copy-start.1
  0.9 0.7 %copy-done.1 = s32[1,6]{1,0:T(1,128)S(1)} copy-done((s32[1,6]{1,0:T(1,128)S(1)}, s32[1,6]{1,0:T(1,128)}, u32[]{:S(2)}) %copy-start.1) | copy-done | bytes 48
  1.6 32.4 %shard_map.37 = (f32[128,768]{1,0:T(8,128)S(1)}, f32[128,768]{1,0:T(8,128)S(1)}) custom-call(f32[128,768]{1,0:T(8,128)} %s_hbm.1, f32[128,384]{1,0:T(8,128)S(1)} %copy-done, s32[1,6]{1,0:T(1,128)S(1)} %copy-done.1), custom_call_target="tpu_custom_call" | custom-call | tf_op jit(solution)/shard_map/pallas_call | solution.py:381
  34.0 0.8 %mul.3 = f32[128,768]{1,0:T(8,128)} multiply(f32[128,768]{1,0:T(8,128)S(1)} %get-tuple-element.7, f32[128,768]{1,0:T(8,128)S(1)} %get-tuple-element.8) | non-fusion elementwise | flops 98304 | bytes 1179648 | tf_op jit(solution)/shard_map/mul | solution.py:402
Async XLA Ops:
  0.0 0.9 %copy-start = (f32[128,384]{1,0:T(8,128)S(1)}, f32[128,384]{1,0:T(8,128)}, u32[]{:S(2)}) copy-start(f32[128,384]{1,0:T(8,128)} %h_ref.1) | copy-start | bytes 589828
  0.9 0.7 %copy-start.1 = (s32[1,6]{1,0:T(1,128)S(1)}, s32[1,6]{1,0:T(1,128)}, u32[]{:S(2)}) copy-start(s32[1,6]{1,0:T(1,128)} %p_ref.1) | copy-start | bytes 76

commit v3 on v2

--- a/solution.py
+++ b/solution.py
@@ -175,15 +175,6 @@
         forward(X_EDGE, k, edge, edge_x)
         rows = pl.ds(pl.multiple_of(near[k] * W + side * R, R), R)
         put(zcol, rows, mine, edge[k])
-    for k in range(2):
-        z_wait(Z_S, k, snb)
-        forward(X_S, k, snb, snb_x)
-        put(sd.at[k], mine, mine, snb[k, :R])
-    for k in range(2):
-        forward_wait(X_EDGE, k, edge_x)
-        rows = pl.ds(pl.multiple_of(near[k] * W + (1 - side) * R, R), R)
-        put(zcol, rows, other, edge_x[k])
-
     eye = (lax.broadcasted_iota(jnp.int32, (W, R), 0) == lax.broadcasted_iota(jnp.int32, (W, R), 1) + side * R).astype(F32)
 
     def kept(grid, slot, here):
@@ -227,6 +218,14 @@
         for k in range(2):
             z_send(Z_I + t, k, i_out.at[t], i_in.at[t])
         if t == 0:
+            for k in range(2):
+                z_wait(Z_S, k, snb)
+                forward(X_S, k, snb, snb_x)
+                put(sd.at[k], mine, mine, snb[k, :R])
+            for k in range(2):
+                forward_wait(X_EDGE, k, edge_x)
+                rows = pl.ds(pl.multiple_of(near[k] * W + (1 - side) * R, R), R)
+                put(zcol, rows, other, edge_x[k])
             for k in range(2):
                 forward_wait(X_S, k, snb_x)
                 put(sd.at[k], other, other, snb_x[k, :R])

time: 34.9 us -> 35.2 us (level)
  no operation moved by 1% of the time
where the time goes in v3:
time: 35.2 us; the launch traced here: 35.1 us
  Pallas kernels  32.7 us (93%)
  local copies, waits for them, and re-layouts  1.58 us (4%)
  other arithmetic  0.79 us (2%)
    pallas_call x1, Pallas kernels, per_device(): pl.pallas_call(functools.partial(kernel, n), out_shape=(jax.ShapeDtypeStr...  32.7 us
    unnamed x4, local copies, waits for them, and re-layouts  1.58 us
    mul x1, other arithmetic, per_device(): return keep * refined  0.79 us

profile of v3, /device:TPU:0, one launch (start us, length us, event | category | flops | bytes accessed | tf_op | source)
XLA Modules:
  0.0 35.1 jit_solution(9897677777353666576)
XLA Ops:
  0.0 0.0 copy-start
  0.0 0.9 %copy-done = f32[128,384]{1,0:T(8,128)S(1)} copy-done((f32[128,384]{1,0:T(8,128)S(1)}, f32[128,384]{1,0:T(8,128)}, u32[]{:S(2)}) %copy-start) | copy-done | bytes 196632
  0.9 0.0 copy-start.1
  0.9 0.7 %copy-done.1 = s32[1,6]{1,0:T(1,128)S(1)} copy-done((s32[1,6]{1,0:T(1,128)S(1)}, s32[1,6]{1,0:T(1,128)}, u32[]{:S(2)}) %copy-start.1) | copy-done | bytes 48
  1.6 32.7 %shard_map.37 = (f32[128,768]{1,0:T(8,128)S(1)}, f32[128,768]{1,0:T(8,128)S(1)}) custom-call(f32[128,768]{1,0:T(8,128)} %s_hbm.1, f32[128,384]{1,0:T(8,128)S(1)} %copy-done, s32[1,6]{1,0:T(1,128)S(1)} %copy-done.1), custom_call_target="tpu_custom_call" | custom-call | tf_op jit(solution)/shard_map/pallas_call | solution.py:380
  34.3 0.8 %mul.3 = f32[128,768]{1,0:T(8,128)} multiply(f32[128,768]{1,0:T(8,128)S(1)} %get-tuple-element.7, f32[128,768]{1,0:T(8,128)S(1)} %get-tuple-element.8) | non-fusion elementwise | flops 98304 | bytes 1179648 | tf_op jit(solution)/shard_map/mul | solution.py:401
Async XLA Ops:
  0.0 0.9 %copy-start = (f32[128,384]{1,0:T(8,128)S(1)}, f32[128,384]{1,0:T(8,128)}, u32[]{:S(2)}) copy-start(f32[128,384]{1,0:T(8,128)} %h_ref.1) | copy-start | bytes 589828
  0.9 0.7 %copy-start.1 = (s32[1,6]{1,0:T(1,128)S(1)}, s32[1,6]{1,0:T(1,128)}, u32[]{:S(2)}) copy-start(s32[1,6]{1,0:T(1,128)} %p_ref.1) | copy-start | bytes 76
